TPU v7x, 32 devices: a whole 2x2x4 slice. The times are simulated.
32 devices in a mesh: groups: 2 (over y), tm: 4 (over z), chan: 4 (over x, core).
Axes of the slice: x: 2, y: 2, z: 4, core: 2. Of those that a mesh axis runs over, the one named last changes fastest.
Arguments:
- vis: bfloat16 [8, 128, 2, 128], P(('groups', 'chan'), 'tm'), parts along dimension 0, may hold values from -6 to 6
- row_weight: bfloat16 [8, 128, 128, 128], P(('groups', 'chan'), 'tm'), parts along dimension 0, may hold values from -4 to 4
- col_weight: bfloat16 [8, 128, 128, 256], P(('groups', 'chan'), 'tm'), parts along dimension 0, may hold values from -0.5 to 0.5
- w_bin: int32 [8, 128, 1], P(('groups', 'chan'), 'tm'), parts along dimension 0, may hold values from 0 to 3; in each aligned block of 32 rows (0 to 31, 32 to 63, ..., all dimensions but the last counted through in order) at most 16 rows name the same one
- tile_col: int32 [8, 128], P(('groups', 'chan'), 'tm'), parts along dimension 0, may hold values from 0 to 15
- w_kernel: bfloat16 [8, 512, 512], P(('groups', 'tm')), parts along dimension 0, may hold values from -0.25 to 0.25
Outputs:
- grid: float32 [8, 128, 16, 512], P(('groups', 'tm'), 'chan'), parts along dimension 0
There are 2 independent parts, one for each index of `groups`. A program takes and returns all parts, laid end to end along the dimension named above; each array names one. Nothing has to cross between parts.
Inputs may be any that keep to these rules, and one draw needn't show every extreme that they name: `w_bin`: within the blocks of one device (aligned blocks of 32 along the channel-group and block dimensions taken together), no w-plane is named more than 16 times, a bound that some block reaches.
All inputs are finite; a program needn't handle non-finite values.
Results may differ from a plain program's by a relative error of at most 0.0041.
Values may be sent and summed in bfloat16 or wider, within the bound.
No kernel may reach another device: no remote copies, remote signals or barrier semaphores. Data moves between devices by JAX's collectives and lax.ppermute only.
A program may use at most 128 MiB of HBM per device.

v0:
```python
import jax
import jax.numpy as jnp
from jax import lax
from jax.sharding import PartitionSpec as P

QW = 256
GC = 4096


def grid_group(total, weighted, columns, targets):
    patch = jnp.einsum("ghkv,gvq->gkhq", weighted, columns, preferred_element_type=jnp.float32)
    flat = patch.reshape(patch.shape[0], -1)
    return total.at[targets].add(flat, mode="drop")


def weigh_rows(rows, visibility):
    return (
        rows.astype(jnp.float32)[:, None, :, :] * visibility.astype(jnp.float32)[:, :, None, :]
    ).astype(jnp.bfloat16)


def body(vis, row_weight, col_weight, w_bin, tile_col, w_kernel):
    planes = lax.axis_size("tm")
    count = vis.shape[1]
    rows_k = row_weight.shape[2]
    width_v = vis.shape[3]
    width_q = col_weight.shape[3]
    tile_count = GC // QW
    per_plane = 2 * count // planes
    slot_total = planes * per_plane
    turns = 4
    group_len = slot_total // turns
    bins = w_bin[0, :, 0]
    tiles = tile_col[0]
    member = (bins[:, None] == jnp.arange(planes, dtype=jnp.int32)[None, :]).astype(jnp.int32)
    before = jnp.cumsum(member, axis=0) - member
    within = jnp.sum(before * member, axis=1)
    target = bins * per_plane + within
    source = (
        jnp.full((slot_total,), count, jnp.int32).at[target].set(jnp.arange(count, dtype=jnp.int32))
    )
    filled = source < count
    picked = jnp.minimum(source, count - 1)
    slot_tile = jnp.where(filled, tiles[picked], tile_count).reshape(planes, per_plane)
    columns = jnp.take(col_weight[0], picked, axis=0).reshape(planes, per_plane, width_v, width_q)
    start = jnp.zeros((tile_count, rows_k * 2 * width_q), jnp.float32)
    rows_sent = jnp.take(row_weight[0], picked, axis=0).reshape(planes, per_plane, rows_k, width_v)
    vis_sent = jnp.take(vis[0], picked, axis=0).reshape(planes, per_plane, 2, width_v)
    got_rows, got_vis, got_columns, got_tiles = (
        lax.all_to_all(rows_sent, "tm", split_axis=0, concat_axis=0, tiled=True),
        lax.all_to_all(vis_sent, "tm", split_axis=0, concat_axis=0, tiled=True),
        lax.all_to_all(columns, "tm", split_axis=0, concat_axis=0, tiled=True),
        lax.all_to_all(slot_tile, "tm", split_axis=0, concat_axis=0, tiled=True),
    )

    def step_raw(total, group):
        rows, visibility, cols, targets = group
        return (grid_group(total, weigh_rows(rows, visibility), cols, targets), None)

    groups = (
        got_rows.reshape(turns, group_len, rows_k, width_v),
        got_vis.reshape(turns, group_len, 2, width_v),
        got_columns.reshape(turns, group_len, width_v, width_q),
        got_tiles.reshape(turns, group_len),
    )
    total, _ = lax.scan(step_raw, start, groups)
    partial_value = total.reshape(tile_count, rows_k, 2 * width_q)
    share = rows_k // lax.axis_size("chan")
    summed = lax.psum(partial_value, "chan")
    mine = lax.dynamic_slice_in_dim(summed, lax.axis_index("chan") * share, share, 1)
    rounded = mine.astype(jnp.bfloat16)
    result = jnp.einsum("tkq,qr->ktr", rounded, w_kernel[0], preferred_element_type=jnp.float32)
    return result[None]


def solution(mesh):
    in_specs = (
        P(("groups", "chan"), "tm", None, None),
        P(("groups", "chan"), "tm", None, None),
        P(("groups", "chan"), "tm", None, None),
        P(("groups", "chan"), "tm", None),
        P(("groups", "chan"), "tm"),
        P(("groups", "tm"), None, None),
    )
    out_specs = P(("groups", "tm"), "chan", None, None)
    return jax.shard_map(body, mesh=mesh, in_specs=in_specs, out_specs=out_specs, check_vma=False)
```

profile of v0, /device:TPU:0, one launch (start us, length us, event | category | flops | bytes accessed | tf_op | source)
XLA Modules:
  0.0 488.4 jit_solution(4983551968529737838)
XLA Ops:
  5.3 6.3 %all-to-all-start = ((s32[4,1,16]{2,1,0:T(1,128)}), s32[4,1,16]{2,1,0:T(1,128)S(1)}, u32[]{:S(2)}, u32[]{:S(2)}) async-start(s32[4,1,16]{2,1,0:T(1,128)} %bitcast.13), calls=%async_computation | async-start | bytes 4096 | tf_op jit(solution)/shard_map/all_to_all | solution.py:53
  13.8 3.4 gather_fusion.2
  17.2 5.1 %all-to-all-start.3 = ((bf16[4,16,2,128]{3,2,1,0:T(2,128)(2,1)}), bf16[4,16,2,128]{3,2,1,0:T(2,128)(2,1)S(1)}, u32[]{:S(2)}, u32[]{:S(2)}) async-start(bf16[4,16,2,128]{3,2,1,0:T(2,128)(2,1)} %broadcast_select_fusion.2), calls=%async_computation.3 | async-start | bytes 65536 | tf_op jit(solution)/shard_map/all_to_all | solution.py:51
  22.3 3.2 broadcast_select_fusion.1
  25.6 2.4 all-to-all-done.3
  28.0 4.4 all-to-all-start.2
  32.4 2.8 gather_fusion.1
  35.2 6.4 %copy.14 = bf16[64,128,256]{1,2,0:T(8,128)(2,1)} copy(bf16[64,128,256]{2,1,0:T(8,128)(2,1)} %gather_fusion.1) | data formatting | bytes 8388608 | tf_op jit(solution)/shard_map/jit(_take)/gather | solution.py:45
  41.6 4.6 broadcast_select_fusion
  46.2 32.8 %all-to-all-done.2 = bf16[4,16,128,128]{3,2,1,0:T(8,128)(2,1)} async-done(((bf16[4,16,128,128]{3,2,1,0:T(8,128)(2,1)}), bf16[4,16,128,128]{3,2,1,0:T(8,128)(2,1)}, u32[]{:S(2)}, u32[]{:S(2)}) %all-to-all-start.2) | async-done | bytes 2097184 | tf_op jit(solution)/shard_map/all_to_all | solution.py:50
  79.0 5.0 %all-to-all-start.1 = ((bf16[4,16,128,256]{2,3,1,0:T(8,128)(2,1)}), bf16[4,16,128,256]{2,3,1,0:T(8,128)(2,1)}, u32[]{:S(2)}, u32[]{:S(2)}) async-start(bf16[4,16,128,256]{2,3,1,0:T(8,128)(2,1)} %broadcast_select_fusion), calls=%async_computation.1 | async-start | bytes 8388608 | tf_op jit(solution)/shard_map/all_to_all | solution.py:52
  84.0 92.6 %all-to-all-done.1 = bf16[4,16,128,256]{2,3,1,0:T(8,128)(2,1)} async-done(((bf16[4,16,128,256]{2,3,1,0:T(8,128)(2,1)}), bf16[4,16,128,256]{2,3,1,0:T(8,128)(2,1)}, u32[]{:S(2)}, u32[]{:S(2)}) %all-to-all-start.1) | async-done | bytes 4194336 | tf_op jit(solution)/shard_map/all_to_all | solution.py:52
  176.6 2.2 broadcast_in_dim.50
  178.8 224.0 %while.10 = (s32[]{:T(128)}, f32[16,65536]{1,0:T(8,128)}, s32[4,16]{1,0:T(4,128)S(1)}, bf16[4,16,128,256]{2,3,1,0:T(8,128)(2,1)}, bf16[4,16,128,128]{3,2,1,0:T(8...) while((s32[]{:T(128)}, f32[16,65536]{1,0:T(8,128)}, s32[4,16]{1,0:T(4,128)S(1)}, ...), condition=%wide.region_5.6_spmd, body=%wide.region_3.5_spmd.sunk | while | flops 270798912 | bytes 37266200 | solution.py:66
  180.0 3.9 convolution_bitcast_fusion.3
  183.9 7.2 %copy.19 = f32[16,128,2,256]{3,2,1,0:T(2,128)} copy(f32[16,128,2,256]{1,3,2,0:T(8,128)} %convolution_bitcast_fusion.3) | data formatting | bytes 8388608 | tf_op jit(solution)/shard_map/while/body/eval_jaxpr/ghkv,gvq->gkhq/transpose | solution.py:11
  191.1 6.3 %reshape.160 = f32[16,65536]{1,0:T(8,128)} reshape(f32[16,128,2,256]{3,2,1,0:T(2,128)} %copy.19) | data formatting | bytes 8388608 | tf_op jit(solution)/shard_map/while/body/eval_jaxpr/reshape | solution.py:12
  197.4 38.3 %scatter_fusion = f32[16,65536]{1,0:T(8,128)} fusion(f32[16,65536]{1,0:T(8,128)} %get-tuple-element.97, s32[16]{0:T(128)S(1)} %fusion.16, f32[16,65536]{1,0:T(8,128)} %reshape.160), kind=kCustom, calls=%fused_computation.4.clone.1 | custom fusion | flops 1048576 | bytes 12582976 | tf_op jit(solution)/shard_map/while/body/eval_jaxpr/scatter-add | solution.py:13
  236.9 3.9 convolution_bitcast_fusion.3
  240.8 7.2 %copy.19 = f32[16,128,2,256]{3,2,1,0:T(2,128)} copy(f32[16,128,2,256]{1,3,2,0:T(8,128)} %convolution_bitcast_fusion.3) | data formatting | bytes 8388608 | tf_op jit(solution)/shard_map/while/body/eval_jaxpr/ghkv,gvq->gkhq/transpose | solution.py:11
  248.0 6.3 %reshape.160 = f32[16,65536]{1,0:T(8,128)} reshape(f32[16,128,2,256]{3,2,1,0:T(2,128)} %copy.19) | data formatting | bytes 8388608 | tf_op jit(solution)/shard_map/while/body/eval_jaxpr/reshape | solution.py:12
  254.3 36.9 %scatter_fusion = f32[16,65536]{1,0:T(8,128)} fusion(f32[16,65536]{1,0:T(8,128)} %get-tuple-element.97, s32[16]{0:T(128)S(1)} %fusion.16, f32[16,65536]{1,0:T(8,128)} %reshape.160), kind=kCustom, calls=%fused_computation.4.clone.1 | custom fusion | flops 1048576 | bytes 12582976 | tf_op jit(solution)/shard_map/while/body/eval_jaxpr/scatter-add | solution.py:13
  292.4 3.9 convolution_bitcast_fusion.3
  296.3 7.2 %copy.19 = f32[16,128,2,256]{3,2,1,0:T(2,128)} copy(f32[16,128,2,256]{1,3,2,0:T(8,128)} %convolution_bitcast_fusion.3) | data formatting | bytes 8388608 | tf_op jit(solution)/shard_map/while/body/eval_jaxpr/ghkv,gvq->gkhq/transpose | solution.py:11
  303.5 6.3 %reshape.160 = f32[16,65536]{1,0:T(8,128)} reshape(f32[16,128,2,256]{3,2,1,0:T(2,128)} %copy.19) | data formatting | bytes 8388608 | tf_op jit(solution)/shard_map/while/body/eval_jaxpr/reshape | solution.py:12
  309.8 37.1 %scatter_fusion = f32[16,65536]{1,0:T(8,128)} fusion(f32[16,65536]{1,0:T(8,128)} %get-tuple-element.97, s32[16]{0:T(128)S(1)} %fusion.16, f32[16,65536]{1,0:T(8,128)} %reshape.160), kind=kCustom, calls=%fused_computation.4.clone.1 | custom fusion | flops 1048576 | bytes 12582976 | tf_op jit(solution)/shard_map/while/body/eval_jaxpr/scatter-add | solution.py:13
  348.1 3.9 convolution_bitcast_fusion.3
  352.0 7.2 %copy.19 = f32[16,128,2,256]{3,2,1,0:T(2,128)} copy(f32[16,128,2,256]{1,3,2,0:T(8,128)} %convolution_bitcast_fusion.3) | data formatting | bytes 8388608 | tf_op jit(solution)/shard_map/while/body/eval_jaxpr/ghkv,gvq->gkhq/transpose | solution.py:11
  359.2 6.3 %reshape.160 = f32[16,65536]{1,0:T(8,128)} reshape(f32[16,128,2,256]{3,2,1,0:T(2,128)} %copy.19) | data formatting | bytes 8388608 | tf_op jit(solution)/shard_map/while/body/eval_jaxpr/reshape | solution.py:12
  365.6 37.0 %scatter_fusion = f32[16,65536]{1,0:T(8,128)} fusion(f32[16,65536]{1,0:T(8,128)} %get-tuple-element.97, s32[16]{0:T(128)S(1)} %fusion.16, f32[16,65536]{1,0:T(8,128)} %reshape.160), kind=kCustom, calls=%fused_computation.4.clone.1 | custom fusion | flops 1048576 | bytes 12582976 | tf_op jit(solution)/shard_map/while/body/eval_jaxpr/scatter-add | solution.py:13
  402.8 6.5 %copy.17 = f32[2,8,128,512]{3,2,1,0:T(8,128)} copy(f32[2,8,128,512]{3,1,2,0:T(8,128)} %bitcast.63) | data formatting | bytes 8388608
  409.4 76.0 %all-reduce.1 = bf16[16,128,512]{2,1,0:T(8,128)(2,1)} all-reduce(f32[16,128,512]{2,1,0:T(8,128)} %bitcast.66), channel_id=1, replica_groups=mesh['groups'=2,'tm'=4,'chan'=4] {'chan'}, use_global_device_ids=true, to_apply=%region_6.7 | all-reduce | flops 1048576 | bytes 6291456 | tf_op jit(solution)/shard_map/psum | solution.py:69
  (33 shorter events, 15.1 us)
Async XLA Ops:
  0.0 32.4 %copy-start = (bf16[1,32,128,256]{3,2,1,0:T(8,128)(2,1)S(1)}, bf16[1,32,128,256]{3,2,1,0:T(8,128)(2,1)}, u32[]{:S(2)}) copy-start(bf16[1,32,128,256]{3,2,1,0:T(8,128)(2,1)} %param.10) | copy-start | bytes 6291460
  5.3 11.9 %all-to-all-start = ((s32[4,1,16]{2,1,0:T(1,128)}), s32[4,1,16]{2,1,0:T(1,128)S(1)}, u32[]{:S(2)}, u32[]{:S(2)}) async-start(s32[4,1,16]{2,1,0:T(1,128)} %bitcast.13), calls=%async_computation | async-start | bytes 4096 | tf_op jit(solution)/shard_map/all_to_all | solution.py:53
  17.2 10.7 %all-to-all-start.3 = ((bf16[4,16,2,128]{3,2,1,0:T(2,128)(2,1)}), bf16[4,16,2,128]{3,2,1,0:T(2,128)(2,1)S(1)}, u32[]{:S(2)}, u32[]{:S(2)}) async-start(bf16[4,16,2,128]{3,2,1,0:T(2,128)(2,1)} %broadcast_select_fusion.2), calls=%async_computation.3 | async-start | bytes 65536 | tf_op jit(solution)/shard_map/all_to_all | solution.py:51
  28.0 51.0 %all-to-all-start.2 = ((bf16[4,16,128,128]{3,2,1,0:T(8,128)(2,1)}), bf16[4,16,128,128]{3,2,1,0:T(8,128)(2,1)}, u32[]{:S(2)}, u32[]{:S(2)}) async-start(bf16[4,16,128,128]{3,2,1,0:T(8,128)(2,1)} %broadcast_select_fusion.1), calls=%async_computation.2 | async-start | bytes 4194304 | tf_op jit(solution)/shard_map/all_to_all | solution.py:50
  79.0 97.6 %all-to-all-start.1 = ((bf16[4,16,128,256]{2,3,1,0:T(8,128)(2,1)}), bf16[4,16,128,256]{2,3,1,0:T(8,128)(2,1)}, u32[]{:S(2)}, u32[]{:S(2)}) async-start(bf16[4,16,128,256]{2,3,1,0:T(8,128)(2,1)} %broadcast_select_fusion), calls=%async_computation.1 | async-start | bytes 8388608 | tf_op jit(solution)/shard_map/all_to_all | solution.py:52
  409.4 76.0 %copy-start.1 = (bf16[1,512,512]{2,1,0:T(8,128)(2,1)S(1)}, bf16[1,512,512]{2,1,0:T(8,128)(2,1)}, u32[]{:S(2)}) copy-start(bf16[1,512,512]{2,1,0:T(8,128)(2,1)} %param.13) | copy-start | bytes 1572868
where the time goes:
time: 492 us; the launch traced here: 488 us
  other arithmetic  165 us (34%)
  waiting for transfers between devices  128 us (26%)
  local copies, waits for them, and re-layouts  81.2 us (17%)
  blocking collectives  76 us (15%)
  starting transfers between devices  20.9 us (4%)
  matrix products  17.1 us (3%)
    scatter-add x4, other arithmetic, grid_group(): return total.at[targets].add(flat, mode='drop')  149 us
    all_to_all x1, waiting for transfers between devices, body(): lax.all_to_all(columns, 'tm', split_axis=0, concat_axis=0, tiled=True)  92.6 us
    psum x1, blocking collectives, body(): summed = lax.psum(partial_value, 'chan')  76 us
    all_to_all x1, waiting for transfers between devices, body(): lax.all_to_all(rows_sent, 'tm', split_axis=0, concat_axis=0, tiled=True)  32.8 us
    transpose x4, local copies, waits for them, and re-layouts, grid_group(): jnp.einsum('ghkv,gvq->gkhq', weighted, columns, preferred_element_type=jn...  28.8 us
    reshape x4, local copies, waits for them, and re-layouts, grid_group(): flat = patch.reshape(patch.shape[0], -1)  25.2 us
    dot_general x4, matrix products, grid_group(): jnp.einsum('ghkv,gvq->gkhq', weighted, columns, preferred_element_type=jn...  15.7 us
  transfers between devices with their start and end apart: 4, of which 3 were waited for; matrix products, arithmetic and copies ran while one was open for 5% of the time, Pallas kernels for 0%

commit v1 on v0

--- a/solution.py
+++ b/solution.py
@@ -1,6 +1,9 @@
+import functools
 import jax
 import jax.numpy as jnp
 from jax import lax
+from jax.experimental import pallas as pl
+from jax.experimental.pallas import tpu as pltpu
 from jax.sharding import PartitionSpec as P
 
 QW = 256
@@ -19,7 +22,7 @@
     ).astype(jnp.bfloat16)
 
 
-def body(vis, row_weight, col_weight, w_bin, tile_col, w_kernel):
+def raw_body(vis, row_weight, col_weight, w_bin, tile_col, w_kernel):
     planes = lax.axis_size("tm")
     count = vis.shape[1]
     rows_k = row_weight.shape[2]
@@ -73,6 +76,140 @@
     return result[None]
 
 
+def plane_kernel(
+    tile_count, share, halves,
+    meta, vis_a, rows_a, cols_a, vis_b, rows_b, cols_b,
+    own, send, acc,
+):
+    count = vis_a.shape[0]
+    width_q = cols_a.shape[2]
+    plane = meta[0]
+    starts = [pl.multiple_of(meta[1 + d], share) for d in range(halves)]
+    base = 1 + halves
+    acc[...] = jnp.zeros_like(acc)
+
+    def one(block, which, vis, rows, cols):
+        code = meta[base + which * count + block]
+
+        @pl.when(lax.div(code, tile_count) == plane)
+        def _():
+            tile = lax.rem(code, tile_count)
+            weights = jnp.concatenate(
+                [rows[block, pl.ds(start, share), :] for start in starts], axis=0
+            ).astype(jnp.float32)
+            values = vis[block].astype(jnp.float32)
+            weighted = jnp.concatenate(
+                [weights * values[0:1, :], weights * values[1:2, :]], axis=0
+            ).astype(jnp.bfloat16)
+            patch = jnp.dot(weighted, cols[block], preferred_element_type=jnp.float32)
+            height = halves * share
+            acc[tile, :, :width_q] += patch[:height]
+            acc[tile, :, width_q:] += patch[height:]
+
+    def step(block, carry):
+        one(block, 0, vis_a, rows_a, cols_a)
+        one(block, 1, vis_b, rows_b, cols_b)
+        return carry
+
+    lax.fori_loop(0, count, step, 0)
+    own[...] = acc[:, :share, :]
+    for d in range(1, halves):
+        send[d - 1] = acc[:, d * share:(d + 1) * share, :].astype(jnp.bfloat16)
+
+
+def grid_plane(meta, mine, other, tile_count, share, halves):
+    width = 2 * mine[2].shape[2]
+    vmem = pl.BlockSpec(memory_space=pltpu.VMEM)
+    return pl.pallas_call(
+        functools.partial(plane_kernel, tile_count, share, halves),
+        out_shape=(
+            jax.ShapeDtypeStruct((tile_count, share, width), jnp.float32),
+            jax.ShapeDtypeStruct((halves - 1, tile_count, share, width), jnp.bfloat16),
+        ),
+        in_specs=[pl.BlockSpec(memory_space=pltpu.SMEM)] + [vmem] * 6,
+        out_specs=(vmem, vmem),
+        scratch_shapes=[pltpu.VMEM((tile_count, halves * share, width), jnp.float32)],
+        compiler_params=pltpu.CompilerParams(vmem_limit_bytes=24 << 20),
+        name="grid_plane",
+    )(meta, *mine, *other)
+
+
+def finish_kernel(parts, own, *refs):
+    received, kernel, out = refs[:parts], refs[parts], refs[parts + 1]
+    total = own[...]
+    for part in received:
+        total = total + part[...].astype(jnp.float32)
+    tiles, share, width = total.shape
+    rounded = total.astype(jnp.bfloat16).reshape(tiles * share, width)
+    result = jnp.dot(rounded, kernel[...], preferred_element_type=jnp.float32)
+    out[...] = jnp.swapaxes(result.reshape(tiles, share, width), 0, 1)
+
+
+def finish(own, received, kernel):
+    tiles, share, width = own.shape
+    return pl.pallas_call(
+        functools.partial(finish_kernel, len(received)),
+        out_shape=jax.ShapeDtypeStruct((share, tiles, width), jnp.float32),
+        compiler_params=pltpu.CompilerParams(vmem_limit_bytes=16 << 20),
+        name="finish",
+    )(own, *received, kernel)
+
+
+def swap(value, axis, bit):
+    size = lax.axis_size(axis)
+    return lax.ppermute(value, axis, [(i, i ^ bit) for i in range(size)])
+
+
+def dense_body(vis, row_weight, col_weight, w_bin, tile_col, w_kernel):
+    planes, chans = lax.axis_size("tm"), lax.axis_size("chan")
+    rows_k = row_weight.shape[2]
+    tile_count = GC // QW
+    share, halves = rows_k // chans, chans // 2
+    me, time = lax.axis_index("chan"), lax.axis_index("tm")
+    code = w_bin[0, :, 0] * tile_count + tile_col[0]
+    mine = (vis[0], row_weight[0], col_weight[0])
+    other = tuple(swap(value, "chan", 1) for value in mine)
+    codes = jnp.concatenate([code, swap(code, "chan", 1)])
+    starts = jnp.stack([(me ^ (2 * d)) * share for d in range(halves)])
+
+    parts = {}
+    for r in reversed(range(planes)):
+        meta = jnp.concatenate([(time ^ r)[None], starts, codes]).astype(jnp.int32)
+        own, send = grid_plane(meta, mine, other, tile_count, share, halves)
+        pieces = {0: own} | {d: send[d - 1] for d in range(1, halves)}
+        bit = halves // 2
+        while bit:
+            for d in range(bit):
+                got = swap(pieces[d + bit].astype(jnp.bfloat16), "chan", 2 * bit)
+                pieces[d] = pieces[d].astype(jnp.float32) + got.astype(jnp.float32)
+            bit //= 2
+        parts[r] = [pieces[0]]
+
+    def added(values):
+        total = values[0].astype(jnp.float32)
+        for value in values[1:]:
+            total = total + value.astype(jnp.float32)
+        return total
+
+    bit = 1
+    while bit < planes:
+        for r in reversed(range(bit, planes, 2 * bit)):
+            parts[r - bit].append(swap(added(parts[r]).astype(jnp.bfloat16), "tm", bit))
+        bit *= 2
+    return finish(parts[0][0], parts[0][1:], w_kernel[0])[None]
+
+
+def body(vis, row_weight, col_weight, w_bin, tile_col, w_kernel):
+    planes, chans = lax.axis_size("tm"), lax.axis_size("chan")
+    count, _, width_v = vis.shape[1:]
+    rows_k, width_q = row_weight.shape[2], col_weight.shape[3]
+    dense = planes * (GC // QW) * rows_k * 2 * width_q
+    raw = 2 * count * width_v * (rows_k + width_q + 2)
+    powers = planes & (planes - 1) == 0 and chans & (chans - 1) == 0 and chans > 1
+    chosen = dense_body if powers and dense <= 2 * raw else raw_body
+    return chosen(vis, row_weight, col_weight, w_bin, tile_col, w_kernel)
+
+
 def solution(mesh):
     in_specs = (
         P(("groups", "chan"), "tm", None, None),

time: 492 us -> 88.9 us (0.18)
  other arithmetic: 165 us -> 5.68 us
  waiting for transfers between devices: 128 us -> 31.5 us
  blocking collectives: 76 us -> 0 us
  local copies, waits for them, and re-layouts: 81.2 us -> 17.6 us
  Pallas kernels: 0 us -> 19.4 us
  matrix products: 17.1 us -> 0 us
  starting transfers between devices: 20.9 us -> 14.6 us
    scatter-add x4 -> x0, other arithmetic: 149 us -> none  [grid_group(): return total.at[targets].add(flat, mode='drop')]
    all_to_all x4 -> x0, waiting for transfers between devices: 128 us -> none  [the longest x1 92.6 us: body(): lax.all_to_all(columns, 'tm', split_axis=0, concat_axis=0, tiled=True)]
    psum x1 -> x0, blocking collectives: 76 us -> none  [body(): summed = lax.psum(partial_value, 'chan')]
    ppermute x0 -> x11, waiting for transfers between devices: none -> 31.5 us  [swap(): return lax.ppermute(value, axis, [(i, i ^ bit) for i in range(size)])]
    transpose x4 -> x0, local copies, waits for them, and re-layouts: 28.8 us -> none  [grid_group(): jnp.einsum('ghkv,gvq->gkhq', weighted, columns, preferred_element_type=jn...]
    reshape x4 -> x0, local copies, waits for them, and re-layouts: 25.2 us -> none  [grid_group(): flat = patch.reshape(patch.shape[0], -1)]
    all_to_all x4 -> x0, starting transfers between devices: 20.9 us -> none  [the longest x1 6.35 us: body(): lax.all_to_all(slot_tile, 'tm', split_axis=0, concat_axis=0, tiled=True)]
    pallas_call x0 -> x5, Pallas kernels: none -> 19.4 us  [the longest x4 17.9 us: grid_plane(): pl.pallas_call(functools.partial(plane_kernel, tile_count, share, halves)...]
  transfers between devices with their start and end apart: 4 -> 11, of which waited for: 3 -> 5; matrix products, arithmetic and copies ran while one was open for 5% -> 7% of each run, Pallas kernels for 0% -> 16%
where the time goes in v1:
time: 88.9 us
  waiting for transfers between devices  31.5 us (35%)
  Pallas kernels  19.4 us (22%)
  local copies, waits for them, and re-layouts  17.6 us (20%)
  starting transfers between devices  14.6 us (16%)
  other arithmetic  5.68 us (6%)
    ppermute x11, waiting for transfers between devices, swap(): return lax.ppermute(value, axis, [(i, i ^ bit) for i in range(size)])  31.5 us
    pallas_call x4, Pallas kernels, grid_plane(): pl.pallas_call(functools.partial(plane_kernel, tile_count, share, halves)...  17.9 us
    unnamed x42, local copies, waits for them, and re-layouts  17.3 us
    ppermute x11, starting transfers between devices, swap(): return lax.ppermute(value, axis, [(i, i ^ bit) for i in range(size)])  14.6 us
    convert_element_type x3, other arithmetic, dense_body(): parts[r - bit].append(swap(added(parts[r]).astype(jnp.bfloat16), 'tm', bit))  4.83 us
  transfers between devices with their start and end apart: 11, of which 5 were waited for; matrix products, arithmetic and copies ran while one was open for 7% of the time, Pallas kernels for 16%

profile of v1, /device:TPU:0, one launch (start us, length us, event | category | flops | bytes accessed | tf_op | source)
XLA Modules:
  0.0 88.9 jit_solution(16756647604271261362)
XLA Ops:
  0.0 0.5 collective-permute-start.3
  1.0 0.7 bitcast_add_fusion
  1.7 4.3 %collective-permute-done = s32[32]{0:T(128)S(1)} collective-permute-done((s32[32]{0:T(128)S(1)}, s32[32]{0:T(128)S(1)}, u32[]{:S(2)}, u32[]{:S(2)}) %collective-permute-start) | collective-permute-done | bytes 160 | tf_op jit(solution)/shard_map/ppermute | solution.py:160
  6.1 1.0 %copy-done.8 = bf16[32,128,128]{2,1,0:T(8,128)(2,1)} copy-done((bf16[32,128,128]{2,1,0:T(8,128)(2,1)}, bf16[32,128,128]{2,1,0:T(8,128)(2,1)S(1)}, u32[]{:S(2)}) %copy-start.8) | copy-done | bytes 1048600
  7.1 1.3 %copy-done.2 = bf16[32,128,256]{2,1,0:T(8,128)(2,1)} copy-done((bf16[32,128,256]{2,1,0:T(8,128)(2,1)}, bf16[32,128,256]{2,1,0:T(8,128)(2,1)S(1)}, u32[]{:S(2)}) %copy-start.2) | copy-done | bytes 2097176
  8.4 1.6 %copy-done = bf16[1,32,128,256]{3,2,1,0:T(8,128)(2,1)S(1)} copy-done((bf16[1,32,128,256]{3,2,1,0:T(8,128)(2,1)S(1)}, bf16[1,32,128,256]{3,2,1,0:T(8,128)(2,1)}, u32[]{:S(2)}) %copy-start) | copy-done | bytes 2097176
  10.0 1.6 %copy-done.3 = bf16[32,128,256]{2,1,0:T(8,128)(2,1)S(1)} copy-done((bf16[32,128,256]{2,1,0:T(8,128)(2,1)S(1)}, bf16[32,128,256]{2,1,0:T(8,128)(2,1)}, u32[]{:S(2)}) %copy-start.3) | copy-done | bytes 2097176
  11.6 1.2 %copy-done.6 = bf16[1,32,128,128]{3,2,1,0:T(8,128)(2,1)S(1)} copy-done((bf16[1,32,128,128]{3,2,1,0:T(8,128)(2,1)S(1)}, bf16[1,32,128,128]{3,2,1,0:T(8,128)(2,1)}, u32[]{:S(2)}) %copy-start.6) | copy-done | bytes 1048600
  12.8 1.2 %copy-done.9 = bf16[32,128,128]{2,1,0:T(8,128)(2,1)S(1)} copy-done((bf16[32,128,128]{2,1,0:T(8,128)(2,1)S(1)}, bf16[32,128,128]{2,1,0:T(8,128)(2,1)}, u32[]{:S(2)}) %copy-start.9) | copy-done | bytes 1048600
  14.1 0.7 copy-done.19
  14.8 3.9 %grid_plane.7 = (f32[16,32,512]{2,1,0:T(8,128)S(1)}, bf16[1,16,32,512]{3,2,1,0:T(8,128)(2,1)}) custom-call(s32[67]{0:T(128)S(1)} %concatenate.20.meta, bf16[32,2,128]{2,1,0:T(2,128)(2,1)S(1)} %bitcast.31, bf16[32,128,128]{2,1,0:T(8,128)(2,1)S(1)} %bitcast.25, bf16[32,128,256]{2,1,0:T(8,128)(2,1)S(1)} %bitcast.20, ...), custom_call_target="tpu_custom_call" | custom-call | tf_op jit(solution)/shard_map/grid_plane/pallas_call | solution.py:123
  18.7 1.0 %copy-done.16 = f32[16,32,512]{2,1,0:T(8,128)} copy-done((f32[16,32,512]{2,1,0:T(8,128)}, f32[16,32,512]{2,1,0:T(8,128)S(1)}, u32[]{:S(2)}) %copy-start.16) | copy-done | bytes 1048600
  19.7 2.8 %collective-permute-start.8 = (bf16[16,32,512]{2,1,0:T(8,128)(2,1)}, bf16[16,32,512]{2,1,0:T(8,128)(2,1)}, u32[]{:S(2)}, u32[]{:S(2)}) collective-permute-start(bf16[16,32,512]{2,1,0:T(8,128)(2,1)} %bitcast.14), channel_id=1, source_target_pairs={{0,2},{1,3},{2,0},{3,1},{4,6},{5,7},{6,4},{7,5},{8,10},{9,11},{10,... | collective-permute-start | bytes 1572872 | tf_op jit(solution)/shard_map/ppermute | solution.py:160
  22.7 1.6 %copy-done.4 = bf16[32,128,256]{2,1,0:T(8,128)(2,1)S(1)} copy-done((bf16[32,128,256]{2,1,0:T(8,128)(2,1)S(1)}, bf16[32,128,256]{2,1,0:T(8,128)(2,1)}, u32[]{:S(2)}) %copy-start.4) | copy-done | bytes 2097176
  24.3 1.2 %copy-done.10 = bf16[32,128,128]{2,1,0:T(8,128)(2,1)S(1)} copy-done((bf16[32,128,128]{2,1,0:T(8,128)(2,1)S(1)}, bf16[32,128,128]{2,1,0:T(8,128)(2,1)}, u32[]{:S(2)}) %copy-start.10) | copy-done | bytes 1048600
  25.5 6.6 %grid_plane.5 = (f32[16,32,512]{2,1,0:T(8,128)S(1)}, bf16[1,16,32,512]{3,2,1,0:T(8,128)(2,1)}) custom-call(s32[67]{0:T(128)S(1)} %concatenate.18.meta, bf16[32,2,128]{2,1,0:T(2,128)(2,1)S(1)} %bitcast.32, bf16[32,128,128]{2,1,0:T(8,128)(2,1)S(1)} %bitcast.26, bf16[32,128,256]{2,1,0:T(8,128)(2,1)S(1)} %bitcast.21, ...), custom_call_target="tpu_custom_call" | custom-call | tf_op jit(solution)/shard_map/grid_plane/pallas_call | solution.py:123
  32.1 1.0 %copy-done.14 = f32[16,32,512]{2,1,0:T(8,128)} copy-done((f32[16,32,512]{2,1,0:T(8,128)}, f32[16,32,512]{2,1,0:T(8,128)S(1)}, u32[]{:S(2)}) %copy-start.14) | copy-done | bytes 1048600
  33.2 3.4 %grid_plane.6 = (f32[16,32,512]{2,1,0:T(8,128)S(1)}, bf16[1,16,32,512]{3,2,1,0:T(8,128)(2,1)}) custom-call(s32[67]{0:T(128)S(1)} %concatenate.19.meta, bf16[32,2,128]{2,1,0:T(2,128)(2,1)S(1)} %bitcast.33, bf16[32,128,128]{2,1,0:T(8,128)(2,1)S(1)} %bitcast.27, bf16[32,128,256]{2,1,0:T(8,128)(2,1)S(1)} %bitcast.22, ...), custom_call_target="tpu_custom_call" | custom-call | tf_op jit(solution)/shard_map/grid_plane/pallas_call | solution.py:123
  36.6 1.0 %copy-done.12 = f32[16,32,512]{2,1,0:T(8,128)} copy-done((f32[16,32,512]{2,1,0:T(8,128)}, f32[16,32,512]{2,1,0:T(8,128)S(1)}, u32[]{:S(2)}) %copy-start.12) | copy-done | bytes 1048600
  37.6 1.9 %collective-permute-start.7 = (bf16[16,32,512]{2,1,0:T(8,128)(2,1)}, bf16[16,32,512]{2,1,0:T(8,128)(2,1)}, u32[]{:S(2)}, u32[]{:S(2)}) collective-permute-start(bf16[16,32,512]{2,1,0:T(8,128)(2,1)} %bitcast.12), channel_id=1, source_target_pairs={{0,2},{1,3},{2,0},{3,1},{4,6},{5,7},{6,4},{7,5},{8,10},{9,11},{10,... | collective-permute-start | bytes 1572872 | tf_op jit(solution)/shard_map/ppermute | solution.py:160
  39.5 2.0 %add_convert_fusion.1 = bf16[16,32,512]{2,1,0:T(8,128)(2,1)} fusion(f32[16,32,512]{2,1,0:T(8,128)S(1)} %copy-done.17, bf16[16,32,512]{2,1,0:T(8,128)(2,1)} %collective-permute-done.8), kind=kLoop, calls=%fused_computation.1 | loop fusion | flops 786432 | bytes 2097152 | tf_op jit(solution)/shard_map/convert_element_type | solution.py:197
  41.8 1.6 %copy-done.5 = bf16[32,128,256]{2,1,0:T(8,128)(2,1)S(1)} copy-done((bf16[32,128,256]{2,1,0:T(8,128)(2,1)S(1)}, bf16[32,128,256]{2,1,0:T(8,128)(2,1)}, u32[]{:S(2)}) %copy-start.5) | copy-done | bytes 2097176
  43.4 1.2 %copy-done.11 = bf16[32,128,128]{2,1,0:T(8,128)(2,1)S(1)} copy-done((bf16[32,128,128]{2,1,0:T(8,128)(2,1)S(1)}, bf16[32,128,128]{2,1,0:T(8,128)(2,1)}, u32[]{:S(2)}) %copy-start.11) | copy-done | bytes 1048600
  44.7 4.0 %grid_plane.4 = (f32[16,32,512]{2,1,0:T(8,128)S(1)}, bf16[1,16,32,512]{3,2,1,0:T(8,128)(2,1)S(1)}) custom-call(s32[67]{0:T(128)S(1)} %concatenate.17.meta, bf16[32,2,128]{2,1,0:T(2,128)(2,1)S(1)} %bitcast.34, bf16[32,128,128]{2,1,0:T(8,128)(2,1)S(1)} %bitcast.28, bf16[32,128,256]{2,1,0:T(8,128)(2,1)S(1)} %bitcast.23, ...), custom_call_target="tpu_custom_call" | custom-call | tf_op jit(solution)/shard_map/grid_plane/pallas_call | solution.py:123
  48.8 1.3 %add_convert_fusion.2 = bf16[16,32,512]{2,1,0:T(8,128)(2,1)S(1)} fusion(f32[16,32,512]{2,1,0:T(8,128)S(1)} %copy-done.15, bf16[16,32,512]{2,1,0:T(8,128)(2,1)} %collective-permute-done.5), kind=kLoop, calls=%fused_computation.2 | loop fusion | flops 786432 | bytes 2097152 | tf_op jit(solution)/shard_map/convert_element_type | solution.py:197
  50.1 3.8 %collective-permute-start.6 = (bf16[16,32,512]{2,1,0:T(8,128)(2,1)S(1)}, bf16[16,32,512]{2,1,0:T(8,128)(2,1)S(1)}, u32[]{:S(2)}, u32[]{:S(2)}) collective-permute-start(bf16[16,32,512]{2,1,0:T(8,128)(2,1)S(1)} %add_convert_fusion.2), channel_id=1, source_target_pairs={{0,4},{4,0},{8,12},{12,8},{1,5},{5,1},{9,13},{13,9},{2,6},{6,2},{1... | collective-permute-start | bytes 1572872 | tf_op jit(solution)/shard_map/ppermute | solution.py:160
  54.0 5.5 %collective-permute-done.7 = bf16[16,32,512]{2,1,0:T(8,128)(2,1)} collective-permute-done((bf16[16,32,512]{2,1,0:T(8,128)(2,1)}, bf16[16,32,512]{2,1,0:T(8,128)(2,1)}, u32[]{:S(2)}, u32[]{:S(2)}) %collective-permute-start.7) | collective-permute-done | bytes 524320 | tf_op jit(solution)/shard_map/ppermute | solution.py:160
  59.5 1.5 %add_convert_fusion = bf16[16,32,512]{2,1,0:T(8,128)(2,1)S(1)} fusion(bf16[16,32,512]{2,1,0:T(8,128)(2,1)} %collective-permute-done.9, f32[16,32,512]{2,1,0:T(8,128)S(1)} %copy-done.13, bf16[16,32,512]{2,1,0:T(8,128)(2,1)} %collective-permute-done.7), kind=kLoop, calls=%fused_computation | loop fusion | flops 1310720 | bytes 2621440 | tf_op jit(solution)/shard_map/convert_element_type | solution.py:197
  61.0 4.6 %collective-permute-start.10 = (bf16[16,32,512]{2,1,0:T(8,128)(2,1)S(1)}, bf16[16,32,512]{2,1,0:T(8,128)(2,1)S(1)}, u32[]{:S(2)}, u32[]{:S(2)}) collective-permute-start(bf16[16,32,512]{2,1,0:T(8,128)(2,1)S(1)} %add_convert_fusion), channel_id=1, source_target_pairs={{0,8},{4,12},{8,0},{12,4},{1,9},{5,13},{9,1},{13,5},{2,10},{6,14},... | collective-permute-start | bytes 1572872 | tf_op jit(solution)/shard_map/ppermute | solution.py:160
  65.6 3.9 %collective-permute-done.4 = bf16[16,32,512]{2,1,0:T(8,128)(2,1)S(1)} collective-permute-done((bf16[16,32,512]{2,1,0:T(8,128)(2,1)S(1)}, bf16[16,32,512]{2,1,0:T(8,128)(2,1)S(1)}, u32[]{:S(2)}, u32[]{:S(2)}) %collective-permute-start.4) | collective-permute-done | bytes 524320 | tf_op jit(solution)/shard_map/ppermute | solution.py:160
  70.0 17.4 %collective-permute-done.10.refs_1_ = bf16[16,32,512]{2,1,0:T(8,128)(2,1)S(1)} collective-permute-done((bf16[16,32,512]{2,1,0:T(8,128)(2,1)S(1)}, bf16[16,32,512]{2,1,0:T(8,128)(2,1)S(1)}, u32[]{:S(2)}, u32[]{:S(2)}) %collective-permute-start.10) | collective-permute-done | bytes 524320 | tf_op jit(solution)/shard_map/ppermute | solution.py:160
  87.4 1.5 %finish.1 = f32[32,16,512]{2,1,0:T(8,128)} custom-call(f32[16,32,512]{2,1,0:T(8,128)S(1)} %convert_add_fusion.own, bf16[16,32,512]{2,1,0:T(8,128)(2,1)S(1)} %collective-permute-done.6.refs_0_, bf16[16,32,512]{2,1,0:T(8,128)(2,1)S(1)} %collective-permute-done.10.refs_1_, bf16[512,512]{1,0:T(8,128)(2,1)S(1)} %bitcast.29), custom_call_target="tpu_custom_call" | custom-call | tf_op jit(solution)/shard_map/finish/pallas_call | solution.py:150
  (46 shorter events, 1.7 us)
Async XLA Ops:
  0.0 7.1 %collective-permute-start.3 = (bf16[32,128,256]{2,1,0:T(8,128)(2,1)}, bf16[32,128,256]{2,1,0:T(8,128)(2,1)S(1)}, u32[]{:S(2)}, u32[]{:S(2)}) collective-permute-start(bf16[32,128,256]{2,1,0:T(8,128)(2,1)} %bitcast.19), channel_id=1, source_target_pairs={{0,1},{1,0},{2,3},{3,2},{4,5},{5,4},{6,7},{7,6},{8,9},{9,8},{10,11... | collective-permute-start | bytes 6291464 | tf_op jit(solution)/shard_map/ppermute | solution.py:160
  0.5 5.6 %collective-permute-start.2 = (bf16[32,128,128]{2,1,0:T(8,128)(2,1)}, bf16[32,128,128]{2,1,0:T(8,128)(2,1)S(1)}, u32[]{:S(2)}, u32[]{:S(2)}) collective-permute-start(bf16[32,128,128]{2,1,0:T(8,128)(2,1)} %bitcast.24), channel_id=1, source_target_pairs={{0,1},{1,0},{2,3},{3,2},{4,5},{5,4},{6,7},{7,6},{8,9},{9,8},{10,11... | collective-permute-start | bytes 3145736 | tf_op jit(solution)/shard_map/ppermute | solution.py:160
  0.5 5.6 %collective-permute-start.1 = (bf16[32,2,128]{2,1,0:T(2,128)(2,1)}, bf16[32,2,128]{2,1,0:T(2,128)(2,1)S(1)}, u32[]{:S(2)}, u32[]{:S(2)}) collective-permute-start(bf16[32,2,128]{2,1,0:T(2,128)(2,1)} %bitcast.30), channel_id=1, source_target_pairs={{0,1},{1,0},{2,3},{3,2},{4,5},{5,4},{6,7},{7,6},{8,9},{9,8},{10,11... | collective-permute-start | bytes 49160 | tf_op jit(solution)/shard_map/ppermute | solution.py:160
  1.7 4.3 %collective-permute-start = (s32[32]{0:T(128)S(1)}, s32[32]{0:T(128)S(1)}, u32[]{:S(2)}, u32[]{:S(2)}) collective-permute-start(s32[32]{0:T(128)S(1)} %bitcast_add_fusion), channel_id=1, source_target_pairs={{0,1},{1,0},{2,3},{3,2},{4,5},{5,4},{6,7},{7,6},{8,9},{9,8},{10,11... | collective-permute-start | bytes 392 | tf_op jit(solution)/shard_map/ppermute | solution.py:160
  6.1 1.0 %copy-start.8 = (bf16[32,128,128]{2,1,0:T(8,128)(2,1)}, bf16[32,128,128]{2,1,0:T(8,128)(2,1)S(1)}, u32[]{:S(2)}) copy-start(bf16[32,128,128]{2,1,0:T(8,128)(2,1)S(1)} %collective-permute-done.2.rows_b) | copy-start | bytes 3145732
  7.1 1.3 %copy-start.2 = (bf16[32,128,256]{2,1,0:T(8,128)(2,1)}, bf16[32,128,256]{2,1,0:T(8,128)(2,1)S(1)}, u32[]{:S(2)}) copy-start(bf16[32,128,256]{2,1,0:T(8,128)(2,1)S(1)} %collective-permute-done.3.cols_b) | copy-start | bytes 6291460
  8.4 1.6 %copy-start = (bf16[1,32,128,256]{3,2,1,0:T(8,128)(2,1)S(1)}, bf16[1,32,128,256]{3,2,1,0:T(8,128)(2,1)}, u32[]{:S(2)}) copy-start(bf16[1,32,128,256]{3,2,1,0:T(8,128)(2,1)} %param.8) | copy-start | bytes 6291460
  10.0 1.6 %copy-start.3 = (bf16[32,128,256]{2,1,0:T(8,128)(2,1)S(1)}, bf16[32,128,256]{2,1,0:T(8,128)(2,1)}, u32[]{:S(2)}) copy-start(bf16[32,128,256]{2,1,0:T(8,128)(2,1)} %copy-done.2) | copy-start | bytes 6291460
  11.6 1.2 %copy-start.6 = (bf16[1,32,128,128]{3,2,1,0:T(8,128)(2,1)S(1)}, bf16[1,32,128,128]{3,2,1,0:T(8,128)(2,1)}, u32[]{:S(2)}) copy-start(bf16[1,32,128,128]{3,2,1,0:T(8,128)(2,1)} %param.7) | copy-start | bytes 3145732
  12.8 1.2 %copy-start.9 = (bf16[32,128,128]{2,1,0:T(8,128)(2,1)S(1)}, bf16[32,128,128]{2,1,0:T(8,128)(2,1)}, u32[]{:S(2)}) copy-start(bf16[32,128,128]{2,1,0:T(8,128)(2,1)} %copy-done.8) | copy-start | bytes 3145732
  14.1 0.7 copy-start.19
  14.8 7.9 %copy-start.1 = (bf16[1,32,128,256]{3,2,1,0:T(8,128)(2,1)S(1)}, bf16[1,32,128,256]{3,2,1,0:T(8,128)(2,1)}, u32[]{:S(2)}) copy-start(bf16[1,32,128,256]{3,2,1,0:T(8,128)(2,1)} %param.8) | copy-start | bytes 6291460
  14.8 7.9 %copy-start.7 = (bf16[1,32,128,128]{3,2,1,0:T(8,128)(2,1)S(1)}, bf16[1,32,128,128]{3,2,1,0:T(8,128)(2,1)}, u32[]{:S(2)}) copy-start(bf16[1,32,128,128]{3,2,1,0:T(8,128)(2,1)} %param.7) | copy-start | bytes 3145732
  14.8 7.9 %copy-start.20 = (bf16[1,32,2,128]{3,2,1,0:T(2,128)(2,1)S(1)}, bf16[1,32,2,128]{3,2,1,0:T(2,128)(2,1)}, u32[]{:S(2)}) copy-start(bf16[1,32,2,128]{3,2,1,0:T(2,128)(2,1)} %param.6) | copy-start | bytes 49156
  18.6 1.0 %copy-start.16 = (f32[16,32,512]{2,1,0:T(8,128)}, f32[16,32,512]{2,1,0:T(8,128)S(1)}, u32[]{:S(2)}) copy-start(f32[16,32,512]{2,1,0:T(8,128)S(1)} %get-tuple-element.19) | copy-start | bytes 3145732
  19.7 19.9 %collective-permute-start.8 = (bf16[16,32,512]{2,1,0:T(8,128)(2,1)}, bf16[16,32,512]{2,1,0:T(8,128)(2,1)}, u32[]{:S(2)}, u32[]{:S(2)}) collective-permute-start(bf16[16,32,512]{2,1,0:T(8,128)(2,1)} %bitcast.14), channel_id=1, source_target_pairs={{0,2},{1,3},{2,0},{3,1},{4,6},{5,7},{6,4},{7,5},{8,10},{9,11},{10,... | collective-permute-start | bytes 1572872 | tf_op jit(solution)/shard_map/ppermute | solution.py:160
  22.7 1.6 %copy-start.4 = (bf16[32,128,256]{2,1,0:T(8,128)(2,1)S(1)}, bf16[32,128,256]{2,1,0:T(8,128)(2,1)}, u32[]{:S(2)}) copy-start(bf16[32,128,256]{2,1,0:T(8,128)(2,1)} %copy-done.2) | copy-start | bytes 6291460
  24.3 1.2 %copy-start.10 = (bf16[32,128,128]{2,1,0:T(8,128)(2,1)S(1)}, bf16[32,128,128]{2,1,0:T(8,128)(2,1)}, u32[]{:S(2)}) copy-start(bf16[32,128,128]{2,1,0:T(8,128)(2,1)} %copy-done.8) | copy-start | bytes 3145732
  32.1 1.0 %copy-start.14 = (f32[16,32,512]{2,1,0:T(8,128)}, f32[16,32,512]{2,1,0:T(8,128)S(1)}, u32[]{:S(2)}) copy-start(f32[16,32,512]{2,1,0:T(8,128)S(1)} %get-tuple-element.15) | copy-start | bytes 3145732
  33.1 6.4 %copy-start.17 = (f32[16,32,512]{2,1,0:T(8,128)S(1)}, f32[16,32,512]{2,1,0:T(8,128)}, u32[]{:S(2)}) copy-start(f32[16,32,512]{2,1,0:T(8,128)} %copy-done.16) | copy-start | bytes 3145732
  33.1 15.7 %collective-permute-start.5 = (bf16[16,32,512]{2,1,0:T(8,128)(2,1)}, bf16[16,32,512]{2,1,0:T(8,128)(2,1)}, u32[]{:S(2)}, u32[]{:S(2)}) collective-permute-start(bf16[16,32,512]{2,1,0:T(8,128)(2,1)} %bitcast.10), channel_id=1, source_target_pairs={{0,2},{1,3},{2,0},{3,1},{4,6},{5,7},{6,4},{7,5},{8,10},{9,11},{10,... | collective-permute-start | bytes 1572872 | tf_op jit(solution)/shard_map/ppermute | solution.py:160
  36.6 1.0 %copy-start.12 = (f32[16,32,512]{2,1,0:T(8,128)}, f32[16,32,512]{2,1,0:T(8,128)S(1)}, u32[]{:S(2)}) copy-start(f32[16,32,512]{2,1,0:T(8,128)S(1)} %get-tuple-element.17) | copy-start | bytes 3145732
  37.6 21.8 %collective-permute-start.7 = (bf16[16,32,512]{2,1,0:T(8,128)(2,1)}, bf16[16,32,512]{2,1,0:T(8,128)(2,1)}, u32[]{:S(2)}, u32[]{:S(2)}) collective-permute-start(bf16[16,32,512]{2,1,0:T(8,128)(2,1)} %bitcast.12), channel_id=1, source_target_pairs={{0,2},{1,3},{2,0},{3,1},{4,6},{5,7},{6,4},{7,5},{8,10},{9,11},{10,... | collective-permute-start | bytes 1572872 | tf_op jit(solution)/shard_map/ppermute | solution.py:160
  41.6 17.9 %collective-permute-start.9 = (bf16[16,32,512]{2,1,0:T(8,128)(2,1)}, bf16[16,32,512]{2,1,0:T(8,128)(2,1)}, u32[]{:S(2)}, u32[]{:S(2)}) collective-permute-start(bf16[16,32,512]{2,1,0:T(8,128)(2,1)} %add_convert_fusion.1), channel_id=1, source_target_pairs={{0,4},{4,0},{8,12},{12,8},{1,5},{5,1},{9,13},{13,9},{2,6},{6,2},{1... | collective-permute-start | bytes 1572872 | tf_op jit(solution)/shard_map/ppermute | solution.py:160
  41.8 1.6 %copy-start.5 = (bf16[32,128,256]{2,1,0:T(8,128)(2,1)S(1)}, bf16[32,128,256]{2,1,0:T(8,128)(2,1)}, u32[]{:S(2)}) copy-start(bf16[32,128,256]{2,1,0:T(8,128)(2,1)} %copy-done.2) | copy-start | bytes 6291460
  43.4 1.2 %copy-start.11 = (bf16[32,128,128]{2,1,0:T(8,128)(2,1)S(1)}, bf16[32,128,128]{2,1,0:T(8,128)(2,1)}, u32[]{:S(2)}) copy-start(bf16[32,128,128]{2,1,0:T(8,128)(2,1)} %copy-done.8) | copy-start | bytes 3145732
  44.7 4.2 %copy-start.15 = (f32[16,32,512]{2,1,0:T(8,128)S(1)}, f32[16,32,512]{2,1,0:T(8,128)}, u32[]{:S(2)}) copy-start(f32[16,32,512]{2,1,0:T(8,128)} %copy-done.14) | copy-start | bytes 3145732
  48.7 10.8 %copy-start.13 = (f32[16,32,512]{2,1,0:T(8,128)S(1)}, f32[16,32,512]{2,1,0:T(8,128)}, u32[]{:S(2)}) copy-start(f32[16,32,512]{2,1,0:T(8,128)} %copy-done.12) | copy-start | bytes 3145732
  48.7 20.8 %collective-permute-start.4 = (bf16[16,32,512]{2,1,0:T(8,128)(2,1)S(1)}, bf16[16,32,512]{2,1,0:T(8,128)(2,1)S(1)}, u32[]{:S(2)}, u32[]{:S(2)}) collective-permute-start(bf16[16,32,512]{2,1,0:T(8,128)(2,1)S(1)} %bitcast.35), channel_id=1, source_target_pairs={{0,2},{1,3},{2,0},{3,1},{4,6},{5,7},{6,4},{7,5},{8,10},{9,11},{10,... | collective-permute-start | bytes 1572872 | tf_op jit(solution)/shard_map/ppermute | solution.py:160
  50.1 19.8 %collective-permute-start.6 = (bf16[16,32,512]{2,1,0:T(8,128)(2,1)S(1)}, bf16[16,32,512]{2,1,0:T(8,128)(2,1)S(1)}, u32[]{:S(2)}, u32[]{:S(2)}) collective-permute-start(bf16[16,32,512]{2,1,0:T(8,128)(2,1)S(1)} %add_convert_fusion.2), channel_id=1, source_target_pairs={{0,4},{4,0},{8,12},{12,8},{1,5},{5,1},{9,13},{13,9},{2,6},{6,2},{1... | collective-permute-start | bytes 1572872 | tf_op jit(solution)/shard_map/ppermute | solution.py:160
  59.5 27.9 %copy-start.18 = (bf16[1,512,512]{2,1,0:T(8,128)(2,1)S(1)}, bf16[1,512,512]{2,1,0:T(8,128)(2,1)}, u32[]{:S(2)}) copy-start(bf16[1,512,512]{2,1,0:T(8,128)(2,1)} %param.11) | copy-start | bytes 1572868
  61.0 26.4 %collective-permute-start.10 = (bf16[16,32,512]{2,1,0:T(8,128)(2,1)S(1)}, bf16[16,32,512]{2,1,0:T(8,128)(2,1)S(1)}, u32[]{:S(2)}, u32[]{:S(2)}) collective-permute-start(bf16[16,32,512]{2,1,0:T(8,128)(2,1)S(1)} %add_convert_fusion), channel_id=1, source_target_pairs={{0,8},{4,12},{8,0},{12,4},{1,9},{5,13},{9,1},{13,5},{2,10},{6,14},... | collective-permute-start | bytes 1572872 | tf_op jit(solution)/shard_map/ppermute | solution.py:160
